TPU v7x, 512 devices: a 4x2x32 block of a 4x8x32 slice. The times are simulated.
512 devices in a mesh: sweep: 2 (over y), row: 8 (over x, core), col: 32 (over z).
Axes of the slice: x: 4, y: 2, z: 32, core: 2. Of those that a mesh axis runs over, the one named last changes fastest.
The devices are a block of a 4x8x32 slice.
Arguments:
- tokens: bfloat16 [1280, 4096], P(('sweep', 'col'), 'row'), parts along dimension 0, may hold values from -6 to 6
- w_gate: bfloat16 [4096, 14336], P('row', 'col'), may hold values from -0.09375 to 0.09375
- w_up: bfloat16 [4096, 14336], P('row', 'col'), may hold values from -0.09375 to 0.09375
- w_down: bfloat16 [14336, 4096], P('col', 'row'), may hold values from -0.046875 to 0.046875
- cotangent: bfloat16 [1280, 4096], P(('sweep', 'col'), 'row'), parts along dimension 0, may hold values from -6 to 6
- step_rate: float32 [2], P('sweep'), parts along dimension 0, may hold values from 0.05 to 0.3
Outputs:
- out_rows: bfloat16 [1280, 4096], P(('sweep', 'col'), 'row'), parts along dimension 0
- grad_in: bfloat16 [1280, 4096], P(('sweep', 'col'), 'row'), parts along dimension 0
- step_gate: bfloat16 [8192, 14336], P(('sweep', 'row'), 'col'), parts along dimension 0
- step_up: bfloat16 [8192, 14336], P(('sweep', 'row'), 'col'), parts along dimension 0
- step_down: bfloat16 [28672, 4096], P(('sweep', 'col'), 'row'), parts along dimension 0
There are 2 independent parts, one for each index of `sweep`. A program takes and returns all parts, laid end to end along the dimension named above; an argument that names none is the same for every part. Nothing has to cross between parts.
All inputs are finite; a program needn't handle non-finite values.
Results may differ from a plain program's by a relative error of at most 0.0049.
Values may be sent and summed in bfloat16 or wider, within the bound.
No kernel may reach another device: no remote copies, remote signals or barrier semaphores. Data moves between devices by JAX's collectives and lax.ppermute only.
A program may use at most 64 MiB of HBM per device.

v0:
```python
import jax
import jax.numpy as jnp
from jax import lax
from jax.sharding import PartitionSpec as P


def cut_along(value, dim, count):
    before, after = (value.shape[:dim], value.shape[dim + 1 :])
    return jnp.moveaxis(value.reshape(*before, count, -1, *after), dim, 0)


def summed_on_arrival(value, axis, dim):
    count = lax.axis_size(axis)
    parts = lax.all_to_all(cut_along(value, dim, count), axis, 0, 0, tiled=True)
    return jnp.sum(parts, axis=0)


def swiglu_back(back_hidden, gate_val, up_val):
    gate_sig = jax.nn.sigmoid(gate_val)
    activation = gate_val * gate_sig
    back_gate = (back_hidden * up_val * gate_sig * (1.0 + gate_val * (1.0 - gate_sig))).astype(
        jnp.bfloat16
    )
    back_up = (back_hidden * activation).astype(jnp.bfloat16)
    return (back_gate, back_up)


def forward_hidden(gate_val, up_val):
    gate_sig = jax.nn.sigmoid(gate_val)
    return (gate_val * gate_sig * up_val).astype(jnp.bfloat16)


def contract_last(left, right):
    return lax.dot_general(
        left, right, (((1,), (1,)), ((), ())), preferred_element_type=jnp.float32
    )


def contract_first(left, right):
    return lax.dot_general(
        left, right, (((0,), (0,)), ((), ())), preferred_element_type=jnp.float32
    )


def local(tokens, w_gate, w_up, w_down, cotangent, step_rate):
    tokens_all = lax.all_gather(tokens, "col", axis=0, tiled=True)
    hidden_width = w_gate.shape[1]
    w_both = jnp.concatenate([w_gate, w_up], axis=1)
    picked = tokens_all
    summed = summed_on_arrival(
        jnp.dot(picked, w_both, preferred_element_type=jnp.float32), "row", 0
    )
    gate_val = summed[:, :hidden_width]
    up_val = summed[:, hidden_width:]
    hidden = forward_hidden(gate_val, up_val)
    hidden_all = lax.all_gather(hidden, "row", axis=0, tiled=True)
    picked = hidden_all
    branch_out = lax.psum_scatter(
        jnp.dot(picked, w_down, preferred_element_type=jnp.float32),
        "col",
        scatter_dimension=0,
        tiled=True,
    )
    out_rows = (tokens.astype(jnp.float32) + branch_out).astype(jnp.bfloat16)
    cotangent_all = lax.all_gather(cotangent, "col", axis=0, tiled=True)
    picked = cotangent_all
    back_hidden = lax.psum_scatter(
        contract_last(picked, w_down), "row", scatter_dimension=0, tiled=True
    )
    back_gate, back_up = swiglu_back(back_hidden, gate_val, up_val)
    gate_grad_all, up_grad_all = (
        lax.all_gather(back_gate, "row", axis=0, tiled=True),
        lax.all_gather(back_up, "row", axis=0, tiled=True),
    )
    grads_all = jnp.concatenate([gate_grad_all, up_grad_all], axis=1)
    picked = grads_all
    input_sums = lax.psum_scatter(
        contract_last(picked, w_both), "col", scatter_dimension=0, tiled=True
    )
    grad_in = (cotangent.astype(jnp.float32) + input_sums).astype(jnp.bfloat16)
    factor = -step_rate[0]
    weight_grads = contract_first(tokens_all, grads_all)
    step_gate = (factor * weight_grads[:, :hidden_width]).astype(jnp.bfloat16)
    step_up = (factor * weight_grads[:, hidden_width:]).astype(jnp.bfloat16)
    step_down = (factor * contract_first(hidden_all, cotangent_all)).astype(jnp.bfloat16)
    return (out_rows, grad_in, step_gate, step_up, step_down)


def solution(mesh):
    in_specs = (
        P(("sweep", "col"), "row"),
        P("row", "col"),
        P("row", "col"),
        P("col", "row"),
        P(("sweep", "col"), "row"),
        P("sweep"),
    )
    out_specs = (
        P(("sweep", "col"), "row"),
        P(("sweep", "col"), "row"),
        P(("sweep", "row"), "col"),
        P(("sweep", "row"), "col"),
        P(("sweep", "col"), "row"),
    )
    return jax.shard_map(local, mesh=mesh, in_specs=in_specs, out_specs=out_specs, check_vma=False)
```

profile of v0, /device:TPU:40, one launch (start us, length us, event | category | flops | bytes accessed | tf_op | source)
XLA Modules:
  0.0 388.1 jit_solution(322608121071958712)
XLA Ops:
  7.2 0.0 copy-start
  7.2 0.1 reduce-scatter.6.cloned.1.call-start
  7.3 99.7 %all-gather.1 = bf16[32,20,512]{2,1,0:T(8,128)(2,1)S(1)} all-gather(bf16[1,20,512]{2,1,0:T(8,128)(2,1)} %bitcast.24), channel_id=1, replica_groups=mesh['sweep'=2,'row'=8,'col'=32] {'col'}, dimensions={0}, use_global_device_ids=true | all-gather | bytes 675840 | tf_op jit(solution)/shard_map/all_gather | solution.py:65
  106.9 0.1 reshape.18
  107.1 0.0 copy-start.7
  107.1 1.6 fusion.14
  108.7 0.1 reduce-scatter.6.cloned.1.call-update
  108.8 0.0 copy-start.8
  108.8 0.6 copy-done.10
  109.5 55.4 %all-gather = bf16[32,20,512]{2,1,0:T(8,128)(2,1)S(1)} all-gather(bf16[1,20,512]{2,1,0:T(8,128)(2,1)S(1)} %bitcast.25), channel_id=1, replica_groups=mesh['sweep'=2,'row'=8,'col'=32] {'col'}, dimensions={0}, use_global_device_ids=true | all-gather | bytes 675840 | tf_op jit(solution)/shard_map/all_gather | solution.py:46
  164.9 0.1 reshape.16
  165.1 2.3 fusion.12
  167.4 4.6 %all-to-all-start = ((f32[8,80,896]{2,1,0:T(8,128)}), f32[8,80,896]{2,1,0:T(8,128)S(1)}, u32[]{:S(2)}, u32[]{:S(2)}) async-start(f32[8,80,896]{2,1,0:T(8,128)} %bitcast.2), calls=%async_computation | async-start | bytes 4587520 | tf_op jit(solution)/shard_map/all_to_all | solution.py:14
  172.7 1.3 dynamic-slice.6
  174.6 26.7 %all-to-all-done = f32[8,80,896]{2,1,0:T(8,128)S(1)} async-done(((f32[8,80,896]{2,1,0:T(8,128)}), f32[8,80,896]{2,1,0:T(8,128)S(1)}, u32[]{:S(2)}, u32[]{:S(2)}) %all-to-all-start) | async-done | bytes 2293792 | tf_op jit(solution)/shard_map/all_to_all | solution.py:14
  201.3 0.8 reduce_sum.9
  202.1 1.2 multiply_convert_fusion.1
  203.3 13.3 %all_gather.18 = bf16[640,448]{1,0:T(8,128)(2,1)S(1)} all-gather(bf16[80,448]{1,0:T(8,128)(2,1)S(1)} %get-tuple-element.11), channel_id=1, replica_groups=mesh['sweep'=2,'row'=8,'col'=32] {'row'}, dimensions={0}, use_global_device_ids=true | all-gather | bytes 645120 | tf_op jit(solution)/shard_map/all_gather | solution.py:72
  216.6 13.3 %all_gather.19 = bf16[640,448]{1,0:T(8,128)(2,1)S(1)} all-gather(bf16[80,448]{1,0:T(8,128)(2,1)S(1)} %get-tuple-element.12), channel_id=1, replica_groups=mesh['sweep'=2,'row'=8,'col'=32] {'row'}, dimensions={0}, use_global_device_ids=true | all-gather | bytes 645120 | tf_op jit(solution)/shard_map/all_gather | solution.py:73
  229.9 13.4 %all_gather.16 = bf16[640,448]{1,0:T(8,128)(2,1)S(1)} all-gather(bf16[80,448]{1,0:T(8,128)(2,1)S(1)} %get-tuple-element.13), channel_id=1, replica_groups=mesh['sweep'=2,'row'=8,'col'=32] {'row'}, dimensions={0}, use_global_device_ids=true | all-gather | bytes 645120 | tf_op jit(solution)/shard_map/all_gather | solution.py:56
  243.4 0.5 fusion.13
  243.9 1.9 fusion.5
  245.8 70.9 %fusion.11 = (f32[24,512]{1,0:T(8,128)S(1)}, f32[24,512]{1,0:T(8,128)S(1)}) fusion(f32[640,512]{1,0:T(8,128)S(1)} %fusion.13, f32[640,512]{1,0:T(8,128)} %fusion.5), kind=kCustom, calls=%all-reduce-scatter.2 | all-reduce-scatter fusion | flops 786433 | bytes 2721792
  316.7 5.5 %collective-permute-start.10 = (f32[24,512]{1,0:T(8,128)S(1)}, f32[24,512]{1,0:T(8,128)S(1)}, u32[]{:S(2)}, u32[]{:S(2)}) collective-permute-start(f32[24,512]{1,0:T(8,128)S(1)} %get-tuple-element.8), channel_id=1, source_target_pairs={{0,5},{1,6},{2,7},{3,8},{4,9},{5,10},{6,11},{7,12},{8,13},{9,14},{... | collective-permute-start | bytes 147464
  322.2 4.2 %collective-permute-start.6 = (f32[24,512]{1,0:T(8,128)S(1)}, f32[24,512]{1,0:T(8,128)S(1)}, u32[]{:S(2)}, u32[]{:S(2)}) collective-permute-start(f32[24,512]{1,0:T(8,128)S(1)} %get-tuple-element.8), channel_id=1, source_target_pairs={{0,1},{1,2},{2,3},{3,4},{4,5},{5,6},{6,7},{7,8},{8,9},{9,10},{10,1... | collective-permute-start | bytes 147464
  326.4 2.2 collective-permute-start.7
  328.6 3.1 collective-permute-start.8
  331.7 2.4 convolution_bitcast_fusion
  334.1 3.5 collective-permute-start.11
  337.6 1.2 fusion.3
  338.8 0.2 collective-permute-done.11
  338.9 5.2 %collective-permute-start.9 = (f32[24,512]{1,0:T(8,128)S(1)}, f32[24,512]{1,0:T(8,128)S(1)}, u32[]{:S(2)}, u32[]{:S(2)}) collective-permute-start(f32[24,512]{1,0:T(8,128)S(1)} %get-tuple-element.8), channel_id=1, source_target_pairs={{0,4},{1,5},{2,6},{3,7},{4,8},{5,9},{6,10},{7,11},{8,12},{9,13},{1... | collective-permute-start | bytes 147464
  344.1 9.9 %collective-permute-start.5 = (f32[4,512]{1,0:T(4,128)S(1)}, f32[4,512]{1,0:T(4,128)S(1)}, u32[]{:S(2)}, u32[]{:S(2)}) collective-permute-start(f32[4,512]{1,0:T(4,128)S(1)} %slice.20), channel_id=1, source_target_pairs={{0,6},{1,7},{2,8},{3,9},{4,10},{5,11},{6,12},{7,13},{8,14},{9,15},... | collective-permute-start | bytes 24584
  354.1 1.3 fusion.2
  355.4 2.8 collective-permute-start
  358.2 0.0 collective-permute-done.7
  358.2 6.5 %collective-permute-start.1 = (f32[24,512]{1,0:T(8,128)S(1)}, f32[24,512]{1,0:T(8,128)S(1)}, u32[]{:S(2)}, u32[]{:S(2)}) collective-permute-start(f32[24,512]{1,0:T(8,128)S(1)} %get-tuple-element.7), channel_id=1, source_target_pairs={{0,2},{1,3},{2,4},{3,5},{4,6},{5,7},{6,8},{7,9},{8,10},{9,11},{10,... | collective-permute-start | bytes 147464
  364.8 5.2 %collective-permute-start.2 = (f32[24,512]{1,0:T(8,128)S(1)}, f32[24,512]{1,0:T(8,128)S(1)}, u32[]{:S(2)}, u32[]{:S(2)}) collective-permute-start(f32[24,512]{1,0:T(8,128)S(1)} %get-tuple-element.7), channel_id=1, source_target_pairs={{0,3},{1,4},{2,5},{3,6},{4,7},{5,8},{6,9},{7,10},{8,11},{9,12},{10... | collective-permute-start | bytes 147464
  370.0 0.0 collective-permute-done.9
  370.0 5.0 %collective-permute-start.3 = (f32[24,512]{1,0:T(8,128)S(1)}, f32[24,512]{1,0:T(8,128)S(1)}, u32[]{:S(2)}, u32[]{:S(2)}) collective-permute-start(f32[24,512]{1,0:T(8,128)S(1)} %get-tuple-element.7), channel_id=1, source_target_pairs={{0,4},{1,5},{2,6},{3,7},{4,8},{5,9},{6,10},{7,11},{8,12},{9,13},{1... | collective-permute-start | bytes 147464
  375.0 0.9 concatenate.9
  375.9 0.0 collective-permute-done.5
  375.9 2.1 collective-permute-start.4
  378.0 0.6 fusion.7
  378.7 0.0 collective-permute-done.1
  378.7 1.1 collective-permute-done.4
  379.7 0.8 concatenate.8
  380.6 0.6 fusion.8
  (29 shorter events, 0.1 us)
Async XLA Ops:
  7.2 99.9 %copy-start = (bf16[448,512]{1,0:T(8,128)(2,1)S(1)}, bf16[448,512]{1,0:T(8,128)(2,1)}, u32[]{:S(2)}) copy-start(bf16[448,512]{1,0:T(8,128)(2,1)} %param.9) | copy-start | bytes 1376260
  7.2 194.9 %reduce-scatter.6.cloned.1.call-start = ((), (), s32[]{:S(2)}) async-start(), calls=%async_computation.2 | async-start | bytes 1474560 | tf_op jit(solution)/shard_map/reduce_scatter | solution.py:67
  107.1 1.6 copy-start.3
  107.1 1.7 copy-start.7
  108.7 0.7 copy-start.10
  108.8 56.2 %copy-start.8 = (bf16[512,448]{0,1:T(8,128)(2,1)S(1)}, bf16[512,448]{0,1:T(8,128)(2,1)}, u32[]{:S(2)}) copy-start(bf16[512,448]{0,1:T(8,128)(2,1)} %param.8) | copy-start | bytes 1376260
  165.1 2.3 copy-start.1
  167.4 33.9 %all-to-all-start = ((f32[8,80,896]{2,1,0:T(8,128)}), f32[8,80,896]{2,1,0:T(8,128)S(1)}, u32[]{:S(2)}, u32[]{:S(2)}) async-start(f32[8,80,896]{2,1,0:T(8,128)} %bitcast.2), calls=%async_computation | async-start | bytes 4587520 | tf_op jit(solution)/shard_map/all_to_all | solution.py:14
  216.6 27.2 %copy-start.5 = (bf16[640,448]{1,0:T(8,128)(2,1)}, bf16[640,448]{1,0:T(8,128)(2,1)S(1)}, u32[]{:S(2)}) copy-start(bf16[640,448]{1,0:T(8,128)(2,1)S(1)} %all_gather.18) | copy-start | bytes 1720324
  229.9 13.9 %copy-start.6 = (bf16[640,448]{1,0:T(8,128)(2,1)}, bf16[640,448]{1,0:T(8,128)(2,1)S(1)}, u32[]{:S(2)}) copy-start(bf16[640,448]{1,0:T(8,128)(2,1)S(1)} %all_gather.19) | copy-start | bytes 1720324
  229.9 13.9 %copy-start.2 = (bf16[512,896]{0,1:T(8,128)(2,1)S(1)}, bf16[512,896]{0,1:T(8,128)(2,1)}, u32[]{:S(2)}) copy-start(bf16[512,896]{0,1:T(8,128)(2,1)} %copy-done.1) | copy-start | bytes 2752516
  316.7 27.4 %collective-permute-start.10 = (f32[24,512]{1,0:T(8,128)S(1)}, f32[24,512]{1,0:T(8,128)S(1)}, u32[]{:S(2)}, u32[]{:S(2)}) collective-permute-start(f32[24,512]{1,0:T(8,128)S(1)} %get-tuple-element.8), channel_id=1, source_target_pairs={{0,5},{1,6},{2,7},{3,8},{4,9},{5,10},{6,11},{7,12},{8,13},{9,14},{... | collective-permute-start | bytes 147464
  322.2 33.2 %collective-permute-start.6 = (f32[24,512]{1,0:T(8,128)S(1)}, f32[24,512]{1,0:T(8,128)S(1)}, u32[]{:S(2)}, u32[]{:S(2)}) collective-permute-start(f32[24,512]{1,0:T(8,128)S(1)} %get-tuple-element.8), channel_id=1, source_target_pairs={{0,1},{1,2},{2,3},{3,4},{4,5},{5,6},{6,7},{7,8},{8,9},{9,10},{10,1... | collective-permute-start | bytes 147464
  326.4 31.8 %collective-permute-start.7 = (f32[24,512]{1,0:T(8,128)S(1)}, f32[24,512]{1,0:T(8,128)S(1)}, u32[]{:S(2)}, u32[]{:S(2)}) collective-permute-start(f32[24,512]{1,0:T(8,128)S(1)} %get-tuple-element.8), channel_id=1, source_target_pairs={{0,2},{1,3},{2,4},{3,5},{4,6},{5,7},{6,8},{7,9},{8,10},{9,11},{10,... | collective-permute-start | bytes 147464
  328.6 36.1 %collective-permute-start.8 = (f32[24,512]{1,0:T(8,128)S(1)}, f32[24,512]{1,0:T(8,128)S(1)}, u32[]{:S(2)}, u32[]{:S(2)}) collective-permute-start(f32[24,512]{1,0:T(8,128)S(1)} %get-tuple-element.8), channel_id=1, source_target_pairs={{0,3},{1,4},{2,5},{3,6},{4,7},{5,8},{6,9},{7,10},{8,11},{9,12},{10... | collective-permute-start | bytes 147464
  334.1 20.0 %copy-start.4 = (bf16[640,512]{1,0:T(8,128)(2,1)S(1)}, bf16[640,512]{1,0:T(8,128)(2,1)}, u32[]{:S(2)}) copy-start(bf16[640,512]{1,0:T(8,128)(2,1)} %copy-done.3) | copy-start | bytes 1966084
  334.1 4.8 %collective-permute-start.11 = (f32[4,512]{1,0:T(4,128)S(1)}, f32[4,512]{1,0:T(4,128)S(1)}, u32[]{:S(2)}, u32[]{:S(2)}) collective-permute-start(f32[4,512]{1,0:T(4,128)S(1)} %slice.21), channel_id=1, source_target_pairs={{0,6},{1,7},{2,8},{3,9},{4,10},{5,11},{6,12},{7,13},{8,14},{9,15},... | collective-permute-start | bytes 24584
  338.8 39.3 %copy-start.9 = (bf16[20,512]{1,0:T(8,128)(2,1)S(1)}, bf16[20,512]{1,0:T(8,128)(2,1)}, u32[]{:S(2)}) copy-start(bf16[20,512]{1,0:T(8,128)(2,1)} %param.10) | copy-start | bytes 61444
  338.9 31.0 %collective-permute-start.9 = (f32[24,512]{1,0:T(8,128)S(1)}, f32[24,512]{1,0:T(8,128)S(1)}, u32[]{:S(2)}, u32[]{:S(2)}) collective-permute-start(f32[24,512]{1,0:T(8,128)S(1)} %get-tuple-element.8), channel_id=1, source_target_pairs={{0,4},{1,5},{2,6},{3,7},{4,8},{5,9},{6,10},{7,11},{8,12},{9,13},{1... | collective-permute-start | bytes 147464
  344.1 31.8 %collective-permute-start.5 = (f32[4,512]{1,0:T(4,128)S(1)}, f32[4,512]{1,0:T(4,128)S(1)}, u32[]{:S(2)}, u32[]{:S(2)}) collective-permute-start(f32[4,512]{1,0:T(4,128)S(1)} %slice.20), channel_id=1, source_target_pairs={{0,6},{1,7},{2,8},{3,9},{4,10},{5,11},{6,12},{7,13},{8,14},{9,15},... | collective-permute-start | bytes 24584
  355.4 23.2 %collective-permute-start = (f32[24,512]{1,0:T(8,128)S(1)}, f32[24,512]{1,0:T(8,128)S(1)}, u32[]{:S(2)}, u32[]{:S(2)}) collective-permute-start(f32[24,512]{1,0:T(8,128)S(1)} %get-tuple-element.7), channel_id=1, source_target_pairs={{0,1},{1,2},{2,3},{3,4},{4,5},{5,6},{6,7},{7,8},{8,9},{9,10},{10,1... | collective-permute-start | bytes 147464
  358.2 20.5 %collective-permute-start.1 = (f32[24,512]{1,0:T(8,128)S(1)}, f32[24,512]{1,0:T(8,128)S(1)}, u32[]{:S(2)}, u32[]{:S(2)}) collective-permute-start(f32[24,512]{1,0:T(8,128)S(1)} %get-tuple-element.7), channel_id=1, source_target_pairs={{0,2},{1,3},{2,4},{3,5},{4,6},{5,7},{6,8},{7,9},{8,10},{9,11},{10,... | collective-permute-start | bytes 147464
  364.8 13.9 %collective-permute-start.2 = (f32[24,512]{1,0:T(8,128)S(1)}, f32[24,512]{1,0:T(8,128)S(1)}, u32[]{:S(2)}, u32[]{:S(2)}) collective-permute-start(f32[24,512]{1,0:T(8,128)S(1)} %get-tuple-element.7), channel_id=1, source_target_pairs={{0,3},{1,4},{2,5},{3,6},{4,7},{5,8},{6,9},{7,10},{8,11},{9,12},{10... | collective-permute-start | bytes 147464
  370.0 8.7 %collective-permute-start.3 = (f32[24,512]{1,0:T(8,128)S(1)}, f32[24,512]{1,0:T(8,128)S(1)}, u32[]{:S(2)}, u32[]{:S(2)}) collective-permute-start(f32[24,512]{1,0:T(8,128)S(1)} %get-tuple-element.7), channel_id=1, source_target_pairs={{0,4},{1,5},{2,6},{3,7},{4,8},{5,9},{6,10},{7,11},{8,12},{9,13},{1... | collective-permute-start | bytes 147464
  375.9 3.8 collective-permute-start.4
Sparse Core Ops, SparseCore 0:
  108.9 32.3 reduce-scatter.5
where the time goes:
time: 389 us; the launch traced here: 388 us
  blocking collectives  266 us (68%)
  starting transfers between devices  59.9 us (15%)
  waiting for transfers between devices  28 us (7%)
  between operations  15.7 us (4%)
  matrix products  10 us (3%)
  other arithmetic  4.44 us (1%)
  local copies, waits for them, and re-layouts  3.94 us (1%)
    all_gather x1, blocking collectives, local(): cotangent_all = lax.all_gather(cotangent, 'col', axis=0, tiled=True)  99.7 us
    unnamed x1, blocking collectives  70.9 us
    all_gather x1, blocking collectives, local(): tokens_all = lax.all_gather(tokens, 'col', axis=0, tiled=True)  55.4 us
    unnamed x12, starting transfers between devices  55.2 us
    all_to_all x1, waiting for transfers between devices, summed_on_arrival(): parts = lax.all_to_all(cut_along(value, dim, count), axis, 0, 0, tiled=True)  26.7 us
    all_gather x1, blocking collectives, local(): hidden_all = lax.all_gather(hidden, 'row', axis=0, tiled=True)  13.4 us
    all_gather x1, blocking collectives, local(): lax.all_gather(back_gate, 'row', axis=0, tiled=True)  13.3 us
    all_gather x1, blocking collectives, local(): lax.all_gather(back_up, 'row', axis=0, tiled=True)  13.3 us
  transfers between devices with their start and end apart: 14, of which 3 were waited for; matrix products, arithmetic and copies ran while one was open for 3% of the time, Pallas kernels for 0%

commit v1 on v0

--- a/solution.py
+++ b/solution.py
@@ -43,7 +43,10 @@
 
 
 def local(tokens, w_gate, w_up, w_down, cotangent, step_rate):
-    tokens_all = lax.all_gather(tokens, "col", axis=0, tiled=True)
+    devices = lax.axis_size("col")
+    pieces = jnp.stack([tokens for _ in range(devices)])
+    pieces = lax.all_to_all(pieces, "col", split_axis=0, concat_axis=0)
+    tokens_all = jnp.concatenate(pieces, axis=0)
     hidden_width = w_gate.shape[1]
     w_both = jnp.concatenate([w_gate, w_up], axis=1)
     picked = tokens_all

time: 389 us -> 425 us (1.093)
  starting transfers between devices: 59.9 us -> 109 us
  blocking collectives: 266 us -> 237 us
  waiting for transfers between devices: 28 us -> 42 us
    all_gather x1 -> x0, blocking collectives: 55.4 us -> none  [local(): tokens_all = lax.all_gather(tokens, 'col', axis=0, tiled=True)]
    all_to_all x0 -> x1, starting transfers between devices: none -> 45.8 us  [local(): pieces = lax.all_to_all(pieces, 'col', split_axis=0, concat_axis=0)]
    all_gather x1, blocking collectives: 99.7 us -> 123 us  [local(): cotangent_all = lax.all_gather(cotangent, 'col', axis=0, tiled=True)]
    reduce_scatter x1, waiting for transfers between devices: 0.01 us -> 10.2 us  [local(): lax.psum_scatter(contract_last(picked, w_down), 'row', scatter_dimension=...]
  transfers between devices with their start and end apart: 14 -> 15, of which waited for: 3 -> 4; matrix products, arithmetic and copies ran while one was open for 3% -> 3% of each run, Pallas kernels for 0% -> 0%
where the time goes in v1:
time: 425 us
  blocking collectives  237 us (56%)
  starting transfers between devices  109 us (26%)
  waiting for transfers between devices  42 us (10%)
  between operations  15.7 us (4%)
  matrix products  9.98 us (2%)
  local copies, waits for them, and re-layouts  6.08 us (1%)
  other arithmetic  4.44 us (1%)
    all_gather x1, blocking collectives, local(): cotangent_all = lax.all_gather(cotangent, 'col', axis=0, tiled=True)  123 us
    unnamed x1, blocking collectives  73.9 us
    unnamed x12, starting transfers between devices  58.7 us
    all_to_all x1, starting transfers between devices, local(): pieces = lax.all_to_all(pieces, 'col', split_axis=0, concat_axis=0)  45.8 us
    all_to_all x1, waiting for transfers between devices, summed_on_arrival(): parts = lax.all_to_all(cut_along(value, dim, count), axis, 0, 0, tiled=True)  30.4 us
    all_gather x1, blocking collectives, local(): hidden_all = lax.all_gather(hidden, 'row', axis=0, tiled=True)  13.4 us
    all_gather x1, blocking collectives, local(): lax.all_gather(back_gate, 'row', axis=0, tiled=True)  13.3 us
    all_gather x1, blocking collectives, local(): lax.all_gather(back_up, 'row', axis=0, tiled=True)  13.3 us
  transfers between devices with their start and end apart: 15, of which 4 were waited for; matrix products, arithmetic and copies ran while one was open for 3% of the time, Pallas kernels for 0%

profile of v1, /device:TPU:40, one launch (start us, length us, event | category | flops | bytes accessed | tf_op | source)
XLA Modules:
  0.0 424.5 jit_solution(2573943568639714799)
XLA Ops:
  7.2 0.0 copy-start
  7.2 1.7 stack.2
  8.9 45.8 %all-to-all-start = ((bf16[32,20,512]{2,1,0:T(8,128)(2,1)}), bf16[32,20,512]{2,1,0:T(8,128)(2,1)S(1)}, u32[]{:S(2)}, u32[]{:S(2)}) async-start(bf16[32,20,512]{2,1,0:T(8,128)(2,1)} %stack.2), calls=%async_computation | async-start | bytes 1572864 | tf_op jit(solution)/shard_map/all_to_all | solution.py:48
  54.7 0.1 reduce-scatter.6.cloned.1.call-start
  54.8 123.3 %all-gather = bf16[32,20,512]{2,1,0:T(8,128)(2,1)S(1)} all-gather(bf16[1,20,512]{2,1,0:T(8,128)(2,1)S(1)} %bitcast.23), channel_id=1, replica_groups=mesh['sweep'=2,'row'=8,'col'=32] {'col'}, dimensions={0}, use_global_device_ids=true | all-gather | bytes 675840 | tf_op jit(solution)/shard_map/all_gather | solution.py:68
  178.1 0.1 reshape.22
  178.3 0.0 copy-start.7
  178.3 1.6 fusion.14
  179.9 0.1 reduce-scatter.6.cloned.1.call-update
  180.0 1.1 constant_dynamic-update-slice_fusion
  181.1 0.1 reshape.19
  181.2 2.3 fusion.12
  183.5 4.6 %all-to-all-start.1 = ((f32[8,80,896]{2,1,0:T(8,128)}), f32[8,80,896]{2,1,0:T(8,128)S(1)}, u32[]{:S(2)}, u32[]{:S(2)}) async-start(f32[8,80,896]{2,1,0:T(8,128)} %bitcast.1), calls=%async_computation.1 | async-start | bytes 4587520 | tf_op jit(solution)/shard_map/all_to_all | solution.py:14
  188.7 1.3 dynamic-slice.6
  190.7 30.4 %all-to-all-done.1 = f32[8,80,896]{2,1,0:T(8,128)S(1)} async-done(((f32[8,80,896]{2,1,0:T(8,128)}), f32[8,80,896]{2,1,0:T(8,128)S(1)}, u32[]{:S(2)}, u32[]{:S(2)}) %all-to-all-start.1) | async-done | bytes 2293792 | tf_op jit(solution)/shard_map/all_to_all | solution.py:14
  221.1 0.8 reduce_sum.9
  221.9 10.2 %reduce-scatter.6.cloned.1.call-done = f32[80,448]{1,0:T(8,128)} async-done(((f32[640,448]{1,0:T(8,128)}), f32[80,448]{1,0:T(8,128)}) %reduce-scatter.6.cloned.1.call-update) | async-done | bytes 143376 | tf_op jit(solution)/shard_map/reduce_scatter | solution.py:70
  232.1 1.2 multiply_convert_fusion.1
  233.3 13.3 %all_gather.14 = bf16[640,448]{1,0:T(8,128)(2,1)S(1)} all-gather(bf16[80,448]{1,0:T(8,128)(2,1)S(1)} %get-tuple-element.11), channel_id=1, replica_groups=mesh['sweep'=2,'row'=8,'col'=32] {'row'}, dimensions={0}, use_global_device_ids=true | all-gather | bytes 645120 | tf_op jit(solution)/shard_map/all_gather | solution.py:75
  246.6 13.3 %all_gather.15 = bf16[640,448]{1,0:T(8,128)(2,1)S(1)} all-gather(bf16[80,448]{1,0:T(8,128)(2,1)S(1)} %get-tuple-element.12), channel_id=1, replica_groups=mesh['sweep'=2,'row'=8,'col'=32] {'row'}, dimensions={0}, use_global_device_ids=true | all-gather | bytes 645120 | tf_op jit(solution)/shard_map/all_gather | solution.py:76
  259.9 13.4 %all_gather.12 = bf16[640,448]{1,0:T(8,128)(2,1)S(1)} all-gather(bf16[80,448]{1,0:T(8,128)(2,1)S(1)} %get-tuple-element.13), channel_id=1, replica_groups=mesh['sweep'=2,'row'=8,'col'=32] {'row'}, dimensions={0}, use_global_device_ids=true | all-gather | bytes 645120 | tf_op jit(solution)/shard_map/all_gather | solution.py:59
  273.3 0.5 fusion.13
  273.9 1.9 fusion.5
  275.8 73.9 %fusion.11 = (f32[24,512]{1,0:T(8,128)S(1)}, f32[24,512]{1,0:T(8,128)S(1)}) fusion(f32[640,512]{1,0:T(8,128)S(1)} %fusion.13, f32[640,512]{1,0:T(8,128)} %fusion.5), kind=kCustom, calls=%all-reduce-scatter.2 | all-reduce-scatter fusion | flops 786433 | bytes 2721792
  349.7 6.0 %collective-permute-start.10 = (f32[24,512]{1,0:T(8,128)S(1)}, f32[24,512]{1,0:T(8,128)S(1)}, u32[]{:S(2)}, u32[]{:S(2)}) collective-permute-start(f32[24,512]{1,0:T(8,128)S(1)} %get-tuple-element.8), channel_id=1, source_target_pairs={{0,5},{1,6},{2,7},{3,8},{4,9},{5,10},{6,11},{7,12},{8,13},{9,14},{... | collective-permute-start | bytes 147464
  355.8 3.4 collective-permute-start.6
  359.2 5.1 %collective-permute-start.7 = (f32[24,512]{1,0:T(8,128)S(1)}, f32[24,512]{1,0:T(8,128)S(1)}, u32[]{:S(2)}, u32[]{:S(2)}) collective-permute-start(f32[24,512]{1,0:T(8,128)S(1)} %get-tuple-element.8), channel_id=1, source_target_pairs={{0,2},{1,3},{2,4},{3,5},{4,6},{5,7},{6,8},{7,9},{8,10},{9,11},{10,... | collective-permute-start | bytes 147464
  364.3 6.0 %collective-permute-start.8 = (f32[24,512]{1,0:T(8,128)S(1)}, f32[24,512]{1,0:T(8,128)S(1)}, u32[]{:S(2)}, u32[]{:S(2)}) collective-permute-start(f32[24,512]{1,0:T(8,128)S(1)} %get-tuple-element.8), channel_id=1, source_target_pairs={{0,3},{1,4},{2,5},{3,6},{4,7},{5,8},{6,9},{7,10},{8,11},{9,12},{10... | collective-permute-start | bytes 147464
  370.3 2.4 convolution_bitcast_fusion
  372.7 10.8 %collective-permute-start.11 = (f32[4,512]{1,0:T(4,128)S(1)}, f32[4,512]{1,0:T(4,128)S(1)}, u32[]{:S(2)}, u32[]{:S(2)}) collective-permute-start(f32[4,512]{1,0:T(4,128)S(1)} %slice.21), channel_id=1, source_target_pairs={{0,6},{1,7},{2,8},{3,9},{4,10},{5,11},{6,12},{7,13},{8,14},{9,15},... | collective-permute-start | bytes 24584
  383.5 1.2 fusion.3
  384.7 0.2 collective-permute-done.11
  384.8 3.5 collective-permute-start.9
  388.4 0.0 collective-permute-done.10
  388.4 10.1 %collective-permute-start.5 = (f32[4,512]{1,0:T(4,128)S(1)}, f32[4,512]{1,0:T(4,128)S(1)}, u32[]{:S(2)}, u32[]{:S(2)}) collective-permute-start(f32[4,512]{1,0:T(4,128)S(1)} %slice.20), channel_id=1, source_target_pairs={{0,6},{1,7},{2,8},{3,9},{4,10},{5,11},{6,12},{7,13},{8,14},{9,15},... | collective-permute-start | bytes 24584
  398.5 1.3 fusion.2
  399.8 0.0 collective-permute-done.6
  399.8 1.8 collective-permute-start
  401.6 0.0 collective-permute-done.7
  401.6 3.9 collective-permute-start.1
  405.5 3.5 collective-permute-start.2
  409.1 2.3 collective-permute-start.3
  411.4 0.9 concatenate.9
  412.2 2.2 collective-permute-start.4
  414.5 0.6 fusion.7
  415.1 1.1 collective-permute-done.4
  416.2 0.8 concatenate.8
  417.0 0.6 fusion.8
  (29 shorter events, 0.1 us)
Async XLA Ops:
  7.2 171.1 %copy-start = (bf16[448,512]{1,0:T(8,128)(2,1)S(1)}, bf16[448,512]{1,0:T(8,128)(2,1)}, u32[]{:S(2)}) copy-start(bf16[448,512]{1,0:T(8,128)(2,1)} %param.9) | copy-start | bytes 1376260
  7.2 47.6 %copy-start.8 = (bf16[20,512]{1,0:T(8,128)(2,1)S(1)}, bf16[20,512]{1,0:T(8,128)(2,1)}, u32[]{:S(2)}) copy-start(bf16[20,512]{1,0:T(8,128)(2,1)} %param.10) | copy-start | bytes 61444
  8.9 172.1 %all-to-all-start = ((bf16[32,20,512]{2,1,0:T(8,128)(2,1)}), bf16[32,20,512]{2,1,0:T(8,128)(2,1)S(1)}, u32[]{:S(2)}, u32[]{:S(2)}) async-start(bf16[32,20,512]{2,1,0:T(8,128)(2,1)} %stack.2), calls=%async_computation | async-start | bytes 1572864 | tf_op jit(solution)/shard_map/all_to_all | solution.py:48
  54.7 177.4 %reduce-scatter.6.cloned.1.call-start = ((), (), s32[]{:S(2)}) async-start(), calls=%async_computation.3 | async-start | bytes 1474560 | tf_op jit(solution)/shard_map/reduce_scatter | solution.py:70
  178.3 1.7 copy-start.3
  178.3 1.7 copy-start.7
  181.1 2.4 copy-start.1
  183.5 37.6 %all-to-all-start.1 = ((f32[8,80,896]{2,1,0:T(8,128)}), f32[8,80,896]{2,1,0:T(8,128)S(1)}, u32[]{:S(2)}, u32[]{:S(2)}) async-start(f32[8,80,896]{2,1,0:T(8,128)} %bitcast.1), calls=%async_computation.1 | async-start | bytes 4587520 | tf_op jit(solution)/shard_map/all_to_all | solution.py:14
  246.6 27.2 %copy-start.5 = (bf16[640,448]{1,0:T(8,128)(2,1)}, bf16[640,448]{1,0:T(8,128)(2,1)S(1)}, u32[]{:S(2)}) copy-start(bf16[640,448]{1,0:T(8,128)(2,1)S(1)} %all_gather.14) | copy-start | bytes 1720324
  259.9 13.9 %copy-start.6 = (bf16[640,448]{1,0:T(8,128)(2,1)}, bf16[640,448]{1,0:T(8,128)(2,1)S(1)}, u32[]{:S(2)}) copy-start(bf16[640,448]{1,0:T(8,128)(2,1)S(1)} %all_gather.15) | copy-start | bytes 1720324
  259.9 13.9 %copy-start.2 = (bf16[512,896]{0,1:T(8,128)(2,1)S(1)}, bf16[512,896]{0,1:T(8,128)(2,1)}, u32[]{:S(2)}) copy-start(bf16[512,896]{0,1:T(8,128)(2,1)} %copy-done.1) | copy-start | bytes 2752516
  349.7 38.7 %collective-permute-start.10 = (f32[24,512]{1,0:T(8,128)S(1)}, f32[24,512]{1,0:T(8,128)S(1)}, u32[]{:S(2)}, u32[]{:S(2)}) collective-permute-start(f32[24,512]{1,0:T(8,128)S(1)} %get-tuple-element.8), channel_id=1, source_target_pairs={{0,5},{1,6},{2,7},{3,8},{4,9},{5,10},{6,11},{7,12},{8,13},{9,14},{... | collective-permute-start | bytes 147464
  355.8 44.0 %collective-permute-start.6 = (f32[24,512]{1,0:T(8,128)S(1)}, f32[24,512]{1,0:T(8,128)S(1)}, u32[]{:S(2)}, u32[]{:S(2)}) collective-permute-start(f32[24,512]{1,0:T(8,128)S(1)} %get-tuple-element.8), channel_id=1, source_target_pairs={{0,1},{1,2},{2,3},{3,4},{4,5},{5,6},{6,7},{7,8},{8,9},{9,10},{10,1... | collective-permute-start | bytes 147464
  359.2 42.4 %collective-permute-start.7 = (f32[24,512]{1,0:T(8,128)S(1)}, f32[24,512]{1,0:T(8,128)S(1)}, u32[]{:S(2)}, u32[]{:S(2)}) collective-permute-start(f32[24,512]{1,0:T(8,128)S(1)} %get-tuple-element.8), channel_id=1, source_target_pairs={{0,2},{1,3},{2,4},{3,5},{4,6},{5,7},{6,8},{7,9},{8,10},{9,11},{10,... | collective-permute-start | bytes 147464
  364.3 41.2 %collective-permute-start.8 = (f32[24,512]{1,0:T(8,128)S(1)}, f32[24,512]{1,0:T(8,128)S(1)}, u32[]{:S(2)}, u32[]{:S(2)}) collective-permute-start(f32[24,512]{1,0:T(8,128)S(1)} %get-tuple-element.8), channel_id=1, source_target_pairs={{0,3},{1,4},{2,5},{3,6},{4,7},{5,8},{6,9},{7,10},{8,11},{9,12},{10... | collective-permute-start | bytes 147464
  372.7 25.8 %copy-start.4 = (bf16[640,512]{1,0:T(8,128)(2,1)S(1)}, bf16[640,512]{1,0:T(8,128)(2,1)}, u32[]{:S(2)}) copy-start(bf16[640,512]{1,0:T(8,128)(2,1)} %copy-done.3) | copy-start | bytes 1966084
  372.7 12.1 %collective-permute-start.11 = (f32[4,512]{1,0:T(4,128)S(1)}, f32[4,512]{1,0:T(4,128)S(1)}, u32[]{:S(2)}, u32[]{:S(2)}) collective-permute-start(f32[4,512]{1,0:T(4,128)S(1)} %slice.21), channel_id=1, source_target_pairs={{0,6},{1,7},{2,8},{3,9},{4,10},{5,11},{6,12},{7,13},{8,14},{9,15},... | collective-permute-start | bytes 24584
  384.7 32.4 %copy-start.9 = (bf16[20,512]{1,0:T(8,128)(2,1)S(1)}, bf16[20,512]{1,0:T(8,128)(2,1)}, u32[]{:S(2)}) copy-start(bf16[20,512]{1,0:T(8,128)(2,1)} %param.6) | copy-start | bytes 61444
  384.8 24.2 %collective-permute-start.9 = (f32[24,512]{1,0:T(8,128)S(1)}, f32[24,512]{1,0:T(8,128)S(1)}, u32[]{:S(2)}, u32[]{:S(2)}) collective-permute-start(f32[24,512]{1,0:T(8,128)S(1)} %get-tuple-element.8), channel_id=1, source_target_pairs={{0,4},{1,5},{2,6},{3,7},{4,8},{5,9},{6,10},{7,11},{8,12},{9,13},{1... | collective-permute-start | bytes 147464
  388.4 23.9 %collective-permute-start.5 = (f32[4,512]{1,0:T(4,128)S(1)}, f32[4,512]{1,0:T(4,128)S(1)}, u32[]{:S(2)}, u32[]{:S(2)}) collective-permute-start(f32[4,512]{1,0:T(4,128)S(1)} %slice.20), channel_id=1, source_target_pairs={{0,6},{1,7},{2,8},{3,9},{4,10},{5,11},{6,12},{7,13},{8,14},{9,15},... | collective-permute-start | bytes 24584
  399.8 15.3 %collective-permute-start = (f32[24,512]{1,0:T(8,128)S(1)}, f32[24,512]{1,0:T(8,128)S(1)}, u32[]{:S(2)}, u32[]{:S(2)}) collective-permute-start(f32[24,512]{1,0:T(8,128)S(1)} %get-tuple-element.7), channel_id=1, source_target_pairs={{0,1},{1,2},{2,3},{3,4},{4,5},{5,6},{6,7},{7,8},{8,9},{9,10},{10,1... | collective-permute-start | bytes 147464
  401.6 13.5 %collective-permute-start.1 = (f32[24,512]{1,0:T(8,128)S(1)}, f32[24,512]{1,0:T(8,128)S(1)}, u32[]{:S(2)}, u32[]{:S(2)}) collective-permute-start(f32[24,512]{1,0:T(8,128)S(1)} %get-tuple-element.7), channel_id=1, source_target_pairs={{0,2},{1,3},{2,4},{3,5},{4,6},{5,7},{6,8},{7,9},{8,10},{9,11},{10,... | collective-permute-start | bytes 147464
  405.5 9.6 %collective-permute-start.2 = (f32[24,512]{1,0:T(8,128)S(1)}, f32[24,512]{1,0:T(8,128)S(1)}, u32[]{:S(2)}, u32[]{:S(2)}) collective-permute-start(f32[24,512]{1,0:T(8,128)S(1)} %get-tuple-element.7), channel_id=1, source_target_pairs={{0,3},{1,4},{2,5},{3,6},{4,7},{5,8},{6,9},{7,10},{8,11},{9,12},{10... | collective-permute-start | bytes 147464
  409.1 6.0 %collective-permute-start.3 = (f32[24,512]{1,0:T(8,128)S(1)}, f32[24,512]{1,0:T(8,128)S(1)}, u32[]{:S(2)}, u32[]{:S(2)}) collective-permute-start(f32[24,512]{1,0:T(8,128)S(1)} %get-tuple-element.7), channel_id=1, source_target_pairs={{0,4},{1,5},{2,6},{3,7},{4,8},{5,9},{6,10},{7,11},{8,12},{9,13},{1... | collective-permute-start | bytes 147464
  412.2 4.0 collective-permute-start.4
Sparse Core Ops, SparseCore 0:
  180.1 52.0 reduce-scatter.5
